TPU v7x, 32 devices: a whole 2x2x4 slice. The times are simulated.
32 devices in a mesh: layer: 8 (over y, x, core), latent: 4 (over z).
Axes of the slice: x: 2, y: 2, z: 4, core: 2. Of those that a mesh axis runs over, the one named last changes fastest.
Arguments:
- decoder: bfloat16 [65536, 4, 2304], P(('layer', 'latent')), may hold values from -0.375 to 0.375
- code_index: int32 [4, 128, 64], replicated, may hold values from 0 to 16383, all different within a row
- code_value: bfloat16 [4, 128, 64], replicated, may hold values from 0.19921875 to 4
- bias: float32 [4, 2304], replicated, may hold values from -3 to 3
- target: bfloat16 [4, 128, 2304], replicated, may hold values from -6 to 6
Outputs:
- layer_error: float32 [4], replicated
- grad_decoder: bfloat16 [65536, 4, 2304], P(('layer', 'latent'))
- code_grad: float32 [4, 128, 64], replicated
Inputs may be any that keep to these rules, and one draw needn't show every extreme that they name: `code_index`: the 64 indices of one token in one layer are distinct.
All inputs are finite; a program needn't handle non-finite values.
Results may differ from a plain program's by a relative error of at most 0.0048.
Values may be sent and summed in bfloat16 or wider, within the bound.
No kernel may reach another device: no remote copies, remote signals or barrier semaphores. Data moves between devices by JAX's collectives and lax.ppermute only.
A program may use at most 192 MiB of HBM per device.

v0:
```python
import jax
import jax.numpy as jnp
from jax import lax
from jax.sharding import PartitionSpec as P

D = 2304
LAYERS = 4
TOPK = 64
TOKENS = 128


def build_codes(index_rows, value_rows, offset, slab_width):
    columns = offset + lax.iota(jnp.int32, slab_width)
    matches = index_rows[:, :, None] == columns[None, None, :]
    dense = jnp.sum(jnp.where(matches, value_rows[:, :, None].astype(jnp.float32), 0.0), axis=1)
    return (matches, dense.astype(jnp.bfloat16))


def contract_rows(left, right):
    return lax.dot_general(
        left, right, (((0,), (0,)), ((), ())), preferred_element_type=jnp.float32
    )


def contract_cols(left, right):
    return lax.dot_general(
        left, right, (((1,), (1,)), ((), ())), preferred_element_type=jnp.float32
    )


def on_device(decoder, code_index, code_value, bias, target):
    layer_count = lax.axis_size("layer")
    latent_count = lax.axis_size("latent")
    group_size = layer_count // LAYERS
    slab_width = decoder.shape[0]
    layer_pos = lax.axis_index("layer")
    source = layer_pos // group_size
    offset = (layer_pos % group_size * latent_count + lax.axis_index("latent")) * slab_width
    matches, dense_codes = build_codes(
        lax.dynamic_index_in_dim(code_index, source, 0, keepdims=False),
        lax.dynamic_index_in_dim(code_value, source, 0, keepdims=False),
        offset,
        slab_width,
    )

    def forward_step(target_layer, totals):
        weight_slab = lax.dynamic_index_in_dim(decoder, target_layer, 1, keepdims=False)
        product = jnp.dot(dense_codes, weight_slab, preferred_element_type=jnp.float32)
        return lax.dynamic_update_index_in_dim(totals, product, target_layer, 0)

    partials = jnp.zeros((LAYERS, TOKENS, D), jnp.float32)
    stop_at = LAYERS
    partials = lax.fori_loop(source, stop_at, forward_step, partials)
    recon_sum = lax.psum(partials, ("layer", "latent"))
    residual = recon_sum + bias[:, None, :] - target.astype(jnp.float32)
    layer_error = jnp.mean(residual * residual, axis=(1, 2))
    error_b = residual.astype(jnp.bfloat16)

    def backward_step(target_layer, state_pair):
        grads, code_sums = state_pair
        weight_slab = lax.dynamic_index_in_dim(decoder, target_layer, 1, keepdims=False)
        target_error = lax.dynamic_index_in_dim(error_b, target_layer, 0, keepdims=False)
        grad_block = contract_rows(dense_codes, target_error).astype(jnp.bfloat16)
        grads = lax.dynamic_update_index_in_dim(grads, grad_block, target_layer, 1)
        return (grads, code_sums + contract_cols(target_error, weight_slab))

    start_pair = (
        jnp.zeros(decoder.shape, jnp.bfloat16),
        jnp.zeros((TOKENS, slab_width), jnp.float32),
    )
    grads, code_sums = lax.fori_loop(source, stop_at, backward_step, start_pair)
    picked = jnp.sum(jnp.where(matches, code_sums[:, None, :], 0.0), axis=2)
    code_parts = lax.dynamic_update_index_in_dim(
        jnp.zeros((LAYERS, TOKENS, TOPK), jnp.float32), picked, source, 0
    )
    code_grad = lax.psum(code_parts, ("layer", "latent"))
    return (layer_error, grads, code_grad)


def solution(mesh):
    placed = (P(("layer", "latent"), None, None), P(), P(), P(), P())
    return jax.shard_map(
        on_device,
        mesh=mesh,
        in_specs=placed,
        out_specs=(P(), P(("layer", "latent"), None, None), P()),
        check_vma=False,
    )
```

profile of v0, /device:TPU:0, one launch (start us, length us, event | category | flops | bytes accessed | tf_op | source)
XLA Modules:
  0.0 428.5 jit_solution(2103701920801345203)
XLA Ops:
  7.2 0.0 copy-start
  7.2 0.0 all-reduce.3.cloned.1.call-start
  7.2 25.9 %copy.19 = bf16[2048,4,2304]{2,0,1:T(8,128)(2,1)} copy(bf16[2048,4,2304]{2,1,0:T(4,128)(2,1)} %param.9) | data formatting | bytes 75497472 | tf_op jit(solution)/shard_map/while | solution.py:53
  33.1 0.7 bitcast_convert_fusion
  33.8 0.1 copy.18
  34.0 0.0 copy-done
  34.0 0.1 copy.17
  34.1 9.8 %fusion.21 = bf16[128,2048]{1,0:T(8,128)(2,1)S(1)} fusion(f32[128,64]{1,0:T(8,128)S(1)} %copy.18, s32[2048]{0:T(1024)S(1)} %iota_add_fusion, s32[128,64]{1,0:T(8,128)S(1)} %copy.17), kind=kLoop, calls=%fused_computation.21 | loop fusion | flops 50069504 | bytes 598016 | tf_op jit(solution)/shard_map/reduce_sum | solution.py:15
  43.9 2.6 broadcast_in_dim.51.clone
  46.5 0.0 copy-start.4
  46.5 26.9 %while.22 = (s32[]{:T(128)}, f32[4,128,2304]{2,1,0:T(8,128)}, bf16[2048,4,2304]{2,0,1:T(8,128)(2,1)}, bf16[128,2048]{1,0:T(8,128)(2,1)S(1)}, s32[]{:T(128)}, /*index=5*/s32[]{:T(128)}, s32[]{:T(128)}) while((s32[]{:T(128)}, f32[4,128,2304]{2,1,0:T(8,128)}, bf16[2048,4,2304]{2,0,1:T(8,128)(2,1)}, bf16[128,2048]{1,0:T(8,128)(2,1)S(1)}, ...), condition=%wide.region_2.3_spmd, body=%wide.region_1.2_spmd.sunk | while | flops 1207959552 | bytes 15859839 | solution.py:53
  46.5 5.2 %fusion.37 = f32[1,128,2304]{1,2,0:T(8,128)S(1)} fusion(bf16[128,2048]{1,0:T(8,128)(2,1)S(1)} %get-tuple-element.191, bf16[2048,4,2304]{2,0,1:T(8,128)(2,1)} %get-tuple-element.190, s32[]{:T(128)S(6)} %select_n.53), kind=kOutput, calls=%fused_computation.3.clone.1 | convolution fusion | flops 1207959552 | bytes 11141124 | tf_op jit(solution)/shard_map/while/body/dot_general | solution.py:48
  51.7 0.4 copy.30
  52.1 1.1 constant_dynamic-update-slice_fusion.3
  53.2 5.2 %fusion.37 = f32[1,128,2304]{1,2,0:T(8,128)S(1)} fusion(bf16[128,2048]{1,0:T(8,128)(2,1)S(1)} %get-tuple-element.191, bf16[2048,4,2304]{2,0,1:T(8,128)(2,1)} %get-tuple-element.190, s32[]{:T(128)S(6)} %select_n.53), kind=kOutput, calls=%fused_computation.3.clone.1 | convolution fusion | flops 1207959552 | bytes 11141124 | tf_op jit(solution)/shard_map/while/body/dot_general | solution.py:48
  58.4 0.4 copy.30
  58.8 1.1 constant_dynamic-update-slice_fusion.3
  59.9 5.2 %fusion.37 = f32[1,128,2304]{1,2,0:T(8,128)S(1)} fusion(bf16[128,2048]{1,0:T(8,128)(2,1)S(1)} %get-tuple-element.191, bf16[2048,4,2304]{2,0,1:T(8,128)(2,1)} %get-tuple-element.190, s32[]{:T(128)S(6)} %select_n.53), kind=kOutput, calls=%fused_computation.3.clone.1 | convolution fusion | flops 1207959552 | bytes 11141124 | tf_op jit(solution)/shard_map/while/body/dot_general | solution.py:48
  65.1 0.4 copy.30
  65.5 1.1 constant_dynamic-update-slice_fusion.3
  66.6 5.2 %fusion.37 = f32[1,128,2304]{1,2,0:T(8,128)S(1)} fusion(bf16[128,2048]{1,0:T(8,128)(2,1)S(1)} %get-tuple-element.191, bf16[2048,4,2304]{2,0,1:T(8,128)(2,1)} %get-tuple-element.190, s32[]{:T(128)S(6)} %select_n.53), kind=kOutput, calls=%fused_computation.3.clone.1 | convolution fusion | flops 1207959552 | bytes 11141124 | tf_op jit(solution)/shard_map/while/body/dot_general | solution.py:48
  71.8 0.4 copy.30
  72.2 1.2 constant_dynamic-update-slice_fusion.3
  73.4 0.0 copy-start.2
  73.4 0.0 all-reduce.3.cloned.1.call-update
  73.4 0.0 all-reduce.5.cloned.1.call-start
  73.5 145.7 %all-reduce.3.cloned.1.call-done = f32[4,128,2304]{2,1,0:T(8,128)} async-done(((f32[4,128,2304]{2,1,0:T(8,128)}), f32[4,128,2304]{2,1,0:T(8,128)}) %all-reduce.3.cloned.1.call-update) | async-done | bytes 4718608 | tf_op jit(solution)/shard_map/psum | solution.py:54
  219.2 0.0 copy-done.4
  219.2 4.1 fusion.23
  223.3 0.0 copy-done.2
  223.3 12.5 %broadcast_in_dim.54 = bf16[2048,4,2304]{0,2,1:T(8,128)(2,1)} broadcast(bf16[]{:T(256)} %constant.88.clone.1), dimensions={} | broadcast | bytes 37748736 | tf_op jit(solution)/shard_map/broadcast_in_dim | solution.py:68
  235.8 0.1 broadcast_in_dim.55
  235.9 52.3 %while.23 = (s32[]{:T(128)}, bf16[2048,4,2304]{0,2,1:T(8,128)(2,1)}, f32[128,2048]{1,0:T(8,128)S(1)}, bf16[4,128,2304]{2,1,0:T(8,128)(2,1)S(1)}, bf16[128,2048]{...) while((s32[]{:T(128)}, bf16[2048,4,2304]{0,2,1:T(8,128)(2,1)}, ...), condition=%wide.region_6.7_spmd, body=%wide.region_5.6_spmd.sunk | while | flops 2420899840 | bytes 22677640 | solution.py:71
  236.0 6.1 %fusion.42 = bf16[2048,4,2304]{0,2,1:T(8,128)(2,1)} fusion(bf16[2048,4,2304]{0,2,1:T(8,128)(2,1)} %get-tuple-element.205, s32[]{:T(128)S(6)} %select_n.54, bf16[128,2048]{1,0:T(8,128)(2,1)} %get-tuple-element.217, bf16[4,128,2304]{2,1,0:T(8,128)(2,1)S(1)} %get-tuple-element.216), kind=kOutput, calls=%fused_computation.8.clone.1 | convolution fusion | flops 1212678144 | bytes 10552320 | tf_op jit(solution)/shard_map/while/body/dot_general | solution.py:20
  242.1 6.9 %fusion.43 = f32[128,2048]{1,0:T(8,128)S(1)} fusion(f32[128,2048]{1,0:T(8,128)S(1)} %get-tuple-element.206, bf16[2048,4,2304]{2,0,1:T(8,128)(2,1)} %get-tuple-element.218, s32[]{:T(128)S(6)} %select_n.54, bf16[4,128,2304]{2,1,0:T(8,128)(2,1)S(1)} %get-tuple-element.216), kind=kOutput, calls=%fused_computation.12.clone.1 | convolution fusion | flops 1208221696 | bytes 12125184 | tf_op jit(solution)/shard_map/while/body/dot_general | solution.py:26
  249.0 6.1 %fusion.42 = bf16[2048,4,2304]{0,2,1:T(8,128)(2,1)} fusion(bf16[2048,4,2304]{0,2,1:T(8,128)(2,1)} %get-tuple-element.205, s32[]{:T(128)S(6)} %select_n.54, bf16[128,2048]{1,0:T(8,128)(2,1)} %get-tuple-element.217, bf16[4,128,2304]{2,1,0:T(8,128)(2,1)S(1)} %get-tuple-element.216), kind=kOutput, calls=%fused_computation.8.clone.1 | convolution fusion | flops 1212678144 | bytes 10552320 | tf_op jit(solution)/shard_map/while/body/dot_general | solution.py:20
  255.1 6.9 %fusion.43 = f32[128,2048]{1,0:T(8,128)S(1)} fusion(f32[128,2048]{1,0:T(8,128)S(1)} %get-tuple-element.206, bf16[2048,4,2304]{2,0,1:T(8,128)(2,1)} %get-tuple-element.218, s32[]{:T(128)S(6)} %select_n.54, bf16[4,128,2304]{2,1,0:T(8,128)(2,1)S(1)} %get-tuple-element.216), kind=kOutput, calls=%fused_computation.12.clone.1 | convolution fusion | flops 1208221696 | bytes 12125184 | tf_op jit(solution)/shard_map/while/body/dot_general | solution.py:26
  262.1 6.2 %fusion.42 = bf16[2048,4,2304]{0,2,1:T(8,128)(2,1)} fusion(bf16[2048,4,2304]{0,2,1:T(8,128)(2,1)} %get-tuple-element.205, s32[]{:T(128)S(6)} %select_n.54, bf16[128,2048]{1,0:T(8,128)(2,1)} %get-tuple-element.217, bf16[4,128,2304]{2,1,0:T(8,128)(2,1)S(1)} %get-tuple-element.216), kind=kOutput, calls=%fused_computation.8.clone.1 | convolution fusion | flops 1212678144 | bytes 10552320 | tf_op jit(solution)/shard_map/while/body/dot_general | solution.py:20
  268.3 6.9 %fusion.43 = f32[128,2048]{1,0:T(8,128)S(1)} fusion(f32[128,2048]{1,0:T(8,128)S(1)} %get-tuple-element.206, bf16[2048,4,2304]{2,0,1:T(8,128)(2,1)} %get-tuple-element.218, s32[]{:T(128)S(6)} %select_n.54, bf16[4,128,2304]{2,1,0:T(8,128)(2,1)S(1)} %get-tuple-element.216), kind=kOutput, calls=%fused_computation.12.clone.1 | convolution fusion | flops 1208221696 | bytes 12125184 | tf_op jit(solution)/shard_map/while/body/dot_general | solution.py:26
  275.2 6.1 %fusion.42 = bf16[2048,4,2304]{0,2,1:T(8,128)(2,1)} fusion(bf16[2048,4,2304]{0,2,1:T(8,128)(2,1)} %get-tuple-element.205, s32[]{:T(128)S(6)} %select_n.54, bf16[128,2048]{1,0:T(8,128)(2,1)} %get-tuple-element.217, bf16[4,128,2304]{2,1,0:T(8,128)(2,1)S(1)} %get-tuple-element.216), kind=kOutput, calls=%fused_computation.8.clone.1 | convolution fusion | flops 1212678144 | bytes 10552320 | tf_op jit(solution)/shard_map/while/body/dot_general | solution.py:20
  281.3 6.9 %fusion.43 = f32[128,2048]{1,0:T(8,128)S(1)} fusion(f32[128,2048]{1,0:T(8,128)S(1)} %get-tuple-element.206, bf16[2048,4,2304]{2,0,1:T(8,128)(2,1)} %get-tuple-element.218, s32[]{:T(128)S(6)} %select_n.54, bf16[4,128,2304]{2,1,0:T(8,128)(2,1)S(1)} %get-tuple-element.216), kind=kOutput, calls=%fused_computation.12.clone.1 | convolution fusion | flops 1208221696 | bytes 12125184 | tf_op jit(solution)/shard_map/while/body/dot_general | solution.py:26
  288.2 9.0 %fusion.22 = f32[128,64]{1,0:T(8,128)S(1)} fusion(f32[128,2048]{1,0:T(8,128)S(1)} %get-tuple-element.60, s32[2048]{0:T(1024)S(1)} %iota_add_fusion, s32[128,64]{1,0:T(8,128)S(1)} %copy.17), kind=kLoop, calls=%fused_computation.22 | loop fusion | flops 50323456 | bytes 1122304 | tf_op jit(solution)/shard_map/reduce_sum | solution.py:72
  297.2 0.1 copy.22
  297.4 0.0 copy-start.3
  297.4 0.6 copy-done.3
  298.0 0.0 all-reduce.5.cloned.1.call-update
  298.0 0.5 broadcast_multiply_fusion
  298.6 0.0 copy-start.1
  298.6 57.6 %copy.23 = bf16[2048,4,2304]{2,1,0:T(4,128)(2,1)} copy(bf16[2048,4,2304]{0,2,1:T(8,128)(2,1)} %get-tuple-element.88) | data formatting | bytes 75497472
  356.2 63.9 %all-reduce.5.cloned.1.call-done = f32[4,128,64]{1,2,0:T(8,128)} async-done(((f32[4,128,64]{1,2,0:T(8,128)}), f32[4,128,64]{1,2,0:T(8,128)}) %all-reduce.5.cloned.1.call-update) | async-done | bytes 131088 | tf_op jit(solution)/shard_map/psum | solution.py:76
  420.1 1.6 copy.51
  421.6 0.0 copy-done.1
  (4 shorter events, 0.1 us)
Async XLA Ops:
  7.2 26.8 %copy-start = (s32[4,128,64]{1,2,0:T(8,128)S(1)}, s32[4,128,64]{1,2,0:T(8,128)}, u32[]{:S(2)}) copy-start(s32[4,128,64]{1,2,0:T(8,128)} %param.10) | copy-start | bytes 393220
  7.2 212.0 %all-reduce.3.cloned.1.call-start = ((), (), s32[]{:S(2)}) async-start(), calls=%async_computation | async-start | bytes 9437184 | tf_op jit(solution)/shard_map/psum | solution.py:54
  46.5 172.7 %copy-start.4 = (f32[4,2304]{1,0:T(4,128)S(1)}, f32[4,2304]{1,0:T(4,128)}, u32[]{:S(2)}) copy-start(f32[4,2304]{1,0:T(4,128)} %param.12) | copy-start | bytes 110596
  73.4 149.9 %copy-start.2 = (bf16[128,2048]{1,0:T(8,128)(2,1)}, bf16[128,2048]{1,0:T(8,128)(2,1)S(1)}, u32[]{:S(2)}) copy-start(bf16[128,2048]{1,0:T(8,128)(2,1)S(1)} %get-tuple-element.230) | copy-start | bytes 1572868
  73.4 346.6 %all-reduce.5.cloned.1.call-start = ((), (), s32[]{:S(2)}) async-start(), calls=%async_computation.1 | async-start | bytes 262144 | tf_op jit(solution)/shard_map/psum | solution.py:76
  297.4 0.7 copy-start.3
  298.6 123.1 %copy-start.1 = (s32[4,128,64]{1,2,0:T(8,128)S(1)}, s32[4,128,64]{1,2,0:T(8,128)}, u32[]{:S(2)}) copy-start(s32[4,128,64]{1,2,0:T(8,128)} %param.10) | copy-start | bytes 393220
Sparse Core Ops, SparseCore 0:
  73.5 145.6 all-reduce.2
  298.2 121.8 all-reduce.4
where the time goes:
time: 430 us; the launch traced here: 428 us
  waiting for transfers between devices  210 us (49%)
  local copies, waits for them, and re-layouts  107 us (25%)
  matrix products  73 us (17%)
  other arithmetic  24.2 us (6%)
  between operations  14.2 us (3%)
    psum x1, waiting for transfers between devices, on_device(): recon_sum = lax.psum(partials, ('layer', 'latent'))  146 us
    psum x1, waiting for transfers between devices, on_device(): code_grad = lax.psum(code_parts, ('layer', 'latent'))  63.9 us
    unnamed x12, local copies, waits for them, and re-layouts  59.9 us
    dot_general x4, matrix products, contract_cols(): lax.dot_general(left, right, (((1,), (1,)), ((), ())), preferred_element_...  27.6 us
    while x1, local copies, waits for them, and re-layouts, on_device(): partials = lax.fori_loop(source, stop_at, forward_step, partials)  25.9 us
    dot_general x4, matrix products, contract_rows(): lax.dot_general(left, right, (((0,), (0,)), ((), ())), preferred_element_...  24.6 us
    dot_general x4, matrix products, forward_step(): jnp.dot(dense_codes, weight_slab, preferred_element_type=jnp.float32)  20.9 us
    broadcast_in_dim x1, local copies, waits for them, and re-layouts, on_device(): jnp.zeros(decoder.shape, jnp.bfloat16)  12.5 us
  transfers between devices with their start and end apart: 2, of which 2 were waited for; matrix products, arithmetic and copies ran while one was open for 14% of the time, Pallas kernels for 0%

commit v1 on v0

--- a/solution.py
+++ b/solution.py
@@ -73,7 +73,7 @@
     code_parts = lax.dynamic_update_index_in_dim(
         jnp.zeros((LAYERS, TOKENS, TOPK), jnp.float32), picked, source, 0
     )
-    code_grad = lax.psum(code_parts, ("layer", "latent"))
+    code_grad = jnp.sum(lax.all_gather(code_parts, ("layer", "latent")), axis=0)
     return (layer_error, grads, code_grad)
 
 

time: 430 us -> 369 us (0.86)
  waiting for transfers between devices: 210 us -> 147 us
    psum x1 -> x0, waiting for transfers between devices: 63.9 us -> none  [on_device(): code_grad = lax.psum(code_parts, ('layer', 'latent'))]
    unnamed x12 -> x11, local copies, waits for them, and re-layouts: 59.9 us -> 58.5 us
  transfers between devices with their start and end apart: 2 -> 2, of which waited for: 2 -> 2; matrix products, arithmetic and copies ran while one was open for 14% -> 16% of each run, Pallas kernels for 0% -> 0%
where the time goes in v1:
time: 369 us; the launch traced here: 367 us
  waiting for transfers between devices  147 us (40%)
  local copies, waits for them, and re-layouts  106 us (29%)
  matrix products  73 us (20%)
  other arithmetic  27.3 us (7%)
  between operations  14.2 us (4%)
    psum x1, waiting for transfers between devices, on_device(): recon_sum = lax.psum(partials, ('layer', 'latent'))  146 us
    unnamed x11, local copies, waits for them, and re-layouts  58.5 us
    dot_general x4, matrix products, contract_cols(): lax.dot_general(left, right, (((1,), (1,)), ((), ())), preferred_element_...  27.6 us
    while x1, local copies, waits for them, and re-layouts, on_device(): partials = lax.fori_loop(source, stop_at, forward_step, partials)  25.9 us
    dot_general x4, matrix products, contract_rows(): lax.dot_general(left, right, (((0,), (0,)), ((), ())), preferred_element_...  24.6 us
    dot_general x4, matrix products, forward_step(): jnp.dot(dense_codes, weight_slab, preferred_element_type=jnp.float32)  20.9 us
    broadcast_in_dim x1, local copies, waits for them, and re-layouts, on_device(): jnp.zeros(decoder.shape, jnp.bfloat16)  12.5 us
    reduce_sum x1, other arithmetic, build_codes(): jnp.sum(jnp.where(matches, value_rows[:, :, None].astype(jnp.float32), 0....  9.81 us
  transfers between devices with their start and end apart: 2, of which 2 were waited for; matrix products, arithmetic and copies ran while one was open for 16% of the time, Pallas kernels for 0%

profile of v1, /device:TPU:0, one launch (start us, length us, event | category | flops | bytes accessed | tf_op | source)
XLA Modules:
  0.0 367.1 jit_solution(16275585443682882522)
XLA Ops:
  7.2 0.0 copy-start
  7.2 0.0 all-reduce.2.cloned.1.call-start
  7.2 25.9 %copy.25 = bf16[2048,4,2304]{2,0,1:T(8,128)(2,1)} copy(bf16[2048,4,2304]{2,1,0:T(4,128)(2,1)} %param.9) | data formatting | bytes 75497472 | tf_op jit(solution)/shard_map/while | solution.py:53
  33.1 0.7 bitcast_convert_fusion
  33.8 0.1 copy.24
  34.0 0.0 copy-done
  34.0 0.1 copy.23
  34.1 9.8 %fusion.21 = bf16[128,2048]{1,0:T(8,128)(2,1)S(1)} fusion(f32[128,64]{1,0:T(8,128)S(1)} %copy.24, s32[2048]{0:T(1024)S(1)} %iota_add_fusion, s32[128,64]{1,0:T(8,128)S(1)} %copy.23), kind=kLoop, calls=%fused_computation.21 | loop fusion | flops 50069504 | bytes 598016 | tf_op jit(solution)/shard_map/reduce_sum | solution.py:15
  43.9 2.6 broadcast_in_dim.49.clone
  46.5 0.0 copy-start.4
  46.5 26.9 %while.22 = (s32[]{:T(128)}, f32[4,128,2304]{2,1,0:T(8,128)}, bf16[2048,4,2304]{2,0,1:T(8,128)(2,1)}, bf16[128,2048]{1,0:T(8,128)(2,1)S(1)}, s32[]{:T(128)}, /*index=5*/s32[]{:T(128)}, s32[]{:T(128)}) while((s32[]{:T(128)}, f32[4,128,2304]{2,1,0:T(8,128)}, bf16[2048,4,2304]{2,0,1:T(8,128)(2,1)}, bf16[128,2048]{1,0:T(8,128)(2,1)S(1)}, ...), condition=%wide.region_2.3_spmd, body=%wide.region_1.2_spmd.sunk | while | flops 1207959552 | bytes 15859839 | solution.py:53
  46.5 5.2 %fusion.37 = f32[1,128,2304]{1,2,0:T(8,128)S(1)} fusion(bf16[128,2048]{1,0:T(8,128)(2,1)S(1)} %get-tuple-element.204, bf16[2048,4,2304]{2,0,1:T(8,128)(2,1)} %get-tuple-element.203, s32[]{:T(128)S(6)} %select_n.53), kind=kOutput, calls=%fused_computation.3.clone.1 | convolution fusion | flops 1207959552 | bytes 11141124 | tf_op jit(solution)/shard_map/while/body/dot_general | solution.py:48
  51.7 0.4 copy.37
  52.1 1.1 constant_dynamic-update-slice_fusion.3
  53.2 5.2 %fusion.37 = f32[1,128,2304]{1,2,0:T(8,128)S(1)} fusion(bf16[128,2048]{1,0:T(8,128)(2,1)S(1)} %get-tuple-element.204, bf16[2048,4,2304]{2,0,1:T(8,128)(2,1)} %get-tuple-element.203, s32[]{:T(128)S(6)} %select_n.53), kind=kOutput, calls=%fused_computation.3.clone.1 | convolution fusion | flops 1207959552 | bytes 11141124 | tf_op jit(solution)/shard_map/while/body/dot_general | solution.py:48
  58.4 0.4 copy.37
  58.8 1.1 constant_dynamic-update-slice_fusion.3
  59.9 5.2 %fusion.37 = f32[1,128,2304]{1,2,0:T(8,128)S(1)} fusion(bf16[128,2048]{1,0:T(8,128)(2,1)S(1)} %get-tuple-element.204, bf16[2048,4,2304]{2,0,1:T(8,128)(2,1)} %get-tuple-element.203, s32[]{:T(128)S(6)} %select_n.53), kind=kOutput, calls=%fused_computation.3.clone.1 | convolution fusion | flops 1207959552 | bytes 11141124 | tf_op jit(solution)/shard_map/while/body/dot_general | solution.py:48
  65.1 0.4 copy.37
  65.5 1.1 constant_dynamic-update-slice_fusion.3
  66.6 5.2 %fusion.37 = f32[1,128,2304]{1,2,0:T(8,128)S(1)} fusion(bf16[128,2048]{1,0:T(8,128)(2,1)S(1)} %get-tuple-element.204, bf16[2048,4,2304]{2,0,1:T(8,128)(2,1)} %get-tuple-element.203, s32[]{:T(128)S(6)} %select_n.53), kind=kOutput, calls=%fused_computation.3.clone.1 | convolution fusion | flops 1207959552 | bytes 11141124 | tf_op jit(solution)/shard_map/while/body/dot_general | solution.py:48
  71.8 0.4 copy.37
  72.2 1.2 constant_dynamic-update-slice_fusion.3
  73.4 0.0 copy-start.2
  73.4 0.0 all-reduce.2.cloned.1.call-update
  73.4 0.0 all-gather.2.cloned.1.call-start
  73.5 145.7 %all-reduce.2.cloned.1.call-done = f32[4,128,2304]{2,1,0:T(8,128)} async-done(((f32[4,128,2304]{2,1,0:T(8,128)}), f32[4,128,2304]{2,1,0:T(8,128)}) %all-reduce.2.cloned.1.call-update) | async-done | bytes 4718608 | tf_op jit(solution)/shard_map/psum | solution.py:54
  219.2 0.0 copy-done.4
  219.2 4.1 %fusion.23 = (bf16[4,128,2304]{2,1,0:T(8,128)(2,1)S(1)}, f32[4]{0:T(128)S(1)}) fusion(bf16[4,128,2304]{2,1,0:T(8,128)(2,1)} %param.13, f32[4,128,2304]{2,1,0:T(8,128)} %all-reduce.2.cloned.1.call-done, f32[4,2304]{1,0:T(4,128)S(1)} %copy-done.4), kind=kLoop, calls=%fused_computation.25 | loop fusion | flops 7077884 | bytes 9474064 | tf_op jit(solution)/shard_map/convert_element_type | solution.py:57
  223.3 0.0 copy-done.2
  223.3 12.5 %broadcast_in_dim.52 = bf16[2048,4,2304]{0,2,1:T(8,128)(2,1)} broadcast(bf16[]{:T(256)} %constant.89.clone.1), dimensions={} | broadcast | bytes 37748736 | tf_op jit(solution)/shard_map/broadcast_in_dim | solution.py:68
  235.8 0.1 broadcast_in_dim.53
  235.9 52.3 %while.23 = (s32[]{:T(128)}, bf16[2048,4,2304]{0,2,1:T(8,128)(2,1)}, f32[128,2048]{1,0:T(8,128)S(1)}, bf16[4,128,2304]{2,1,0:T(8,128)(2,1)S(1)}, bf16[128,2048]{...) while((s32[]{:T(128)}, bf16[2048,4,2304]{0,2,1:T(8,128)(2,1)}, ...), condition=%wide.region_6.7_spmd, body=%wide.region_5.6_spmd.sunk | while | flops 2420899840 | bytes 22677640 | solution.py:71
  236.0 6.1 %fusion.42 = bf16[2048,4,2304]{0,2,1:T(8,128)(2,1)} fusion(bf16[2048,4,2304]{0,2,1:T(8,128)(2,1)} %get-tuple-element.218, s32[]{:T(128)S(6)} %select_n.54, bf16[128,2048]{1,0:T(8,128)(2,1)} %get-tuple-element.230, bf16[4,128,2304]{2,1,0:T(8,128)(2,1)S(1)} %get-tuple-element.229), kind=kOutput, calls=%fused_computation.8.clone.1 | convolution fusion | flops 1212678144 | bytes 10552320 | tf_op jit(solution)/shard_map/while/body/dot_general | solution.py:20
  242.1 6.9 %fusion.43 = f32[128,2048]{1,0:T(8,128)S(1)} fusion(f32[128,2048]{1,0:T(8,128)S(1)} %get-tuple-element.219, bf16[2048,4,2304]{2,0,1:T(8,128)(2,1)} %get-tuple-element.231, s32[]{:T(128)S(6)} %select_n.54, bf16[4,128,2304]{2,1,0:T(8,128)(2,1)S(1)} %get-tuple-element.229), kind=kOutput, calls=%fused_computation.12.clone.1 | convolution fusion | flops 1208221696 | bytes 12125184 | tf_op jit(solution)/shard_map/while/body/dot_general | solution.py:26
  249.0 6.1 %fusion.42 = bf16[2048,4,2304]{0,2,1:T(8,128)(2,1)} fusion(bf16[2048,4,2304]{0,2,1:T(8,128)(2,1)} %get-tuple-element.218, s32[]{:T(128)S(6)} %select_n.54, bf16[128,2048]{1,0:T(8,128)(2,1)} %get-tuple-element.230, bf16[4,128,2304]{2,1,0:T(8,128)(2,1)S(1)} %get-tuple-element.229), kind=kOutput, calls=%fused_computation.8.clone.1 | convolution fusion | flops 1212678144 | bytes 10552320 | tf_op jit(solution)/shard_map/while/body/dot_general | solution.py:20
  255.1 6.9 %fusion.43 = f32[128,2048]{1,0:T(8,128)S(1)} fusion(f32[128,2048]{1,0:T(8,128)S(1)} %get-tuple-element.219, bf16[2048,4,2304]{2,0,1:T(8,128)(2,1)} %get-tuple-element.231, s32[]{:T(128)S(6)} %select_n.54, bf16[4,128,2304]{2,1,0:T(8,128)(2,1)S(1)} %get-tuple-element.229), kind=kOutput, calls=%fused_computation.12.clone.1 | convolution fusion | flops 1208221696 | bytes 12125184 | tf_op jit(solution)/shard_map/while/body/dot_general | solution.py:26
  262.1 6.2 %fusion.42 = bf16[2048,4,2304]{0,2,1:T(8,128)(2,1)} fusion(bf16[2048,4,2304]{0,2,1:T(8,128)(2,1)} %get-tuple-element.218, s32[]{:T(128)S(6)} %select_n.54, bf16[128,2048]{1,0:T(8,128)(2,1)} %get-tuple-element.230, bf16[4,128,2304]{2,1,0:T(8,128)(2,1)S(1)} %get-tuple-element.229), kind=kOutput, calls=%fused_computation.8.clone.1 | convolution fusion | flops 1212678144 | bytes 10552320 | tf_op jit(solution)/shard_map/while/body/dot_general | solution.py:20
  268.3 6.9 %fusion.43 = f32[128,2048]{1,0:T(8,128)S(1)} fusion(f32[128,2048]{1,0:T(8,128)S(1)} %get-tuple-element.219, bf16[2048,4,2304]{2,0,1:T(8,128)(2,1)} %get-tuple-element.231, s32[]{:T(128)S(6)} %select_n.54, bf16[4,128,2304]{2,1,0:T(8,128)(2,1)S(1)} %get-tuple-element.229), kind=kOutput, calls=%fused_computation.12.clone.1 | convolution fusion | flops 1208221696 | bytes 12125184 | tf_op jit(solution)/shard_map/while/body/dot_general | solution.py:26
  275.2 6.1 %fusion.42 = bf16[2048,4,2304]{0,2,1:T(8,128)(2,1)} fusion(bf16[2048,4,2304]{0,2,1:T(8,128)(2,1)} %get-tuple-element.218, s32[]{:T(128)S(6)} %select_n.54, bf16[128,2048]{1,0:T(8,128)(2,1)} %get-tuple-element.230, bf16[4,128,2304]{2,1,0:T(8,128)(2,1)S(1)} %get-tuple-element.229), kind=kOutput, calls=%fused_computation.8.clone.1 | convolution fusion | flops 1212678144 | bytes 10552320 | tf_op jit(solution)/shard_map/while/body/dot_general | solution.py:20
  281.3 6.9 %fusion.43 = f32[128,2048]{1,0:T(8,128)S(1)} fusion(f32[128,2048]{1,0:T(8,128)S(1)} %get-tuple-element.219, bf16[2048,4,2304]{2,0,1:T(8,128)(2,1)} %get-tuple-element.231, s32[]{:T(128)S(6)} %select_n.54, bf16[4,128,2304]{2,1,0:T(8,128)(2,1)S(1)} %get-tuple-element.229), kind=kOutput, calls=%fused_computation.12.clone.1 | convolution fusion | flops 1208221696 | bytes 12125184 | tf_op jit(solution)/shard_map/while/body/dot_general | solution.py:26
  288.2 9.0 %fusion.22 = f32[128,64]{1,0:T(8,128)S(1)} fusion(f32[128,2048]{1,0:T(8,128)S(1)} %get-tuple-element.60, s32[2048]{0:T(1024)S(1)} %iota_add_fusion, s32[128,64]{1,0:T(8,128)S(1)} %copy.23), kind=kLoop, calls=%fused_computation.22 | loop fusion | flops 50323456 | bytes 1122304 | tf_op jit(solution)/shard_map/reduce_sum | solution.py:72
  297.2 0.1 copy.28
  297.4 0.0 copy-start.3
  297.4 0.6 copy-done.3
  298.0 0.0 all-gather.2.cloned.1.call-update
  298.0 0.0 copy-start.1
  298.1 57.9 %copy.29 = bf16[2048,4,2304]{2,1,0:T(4,128)(2,1)} copy(bf16[2048,4,2304]{0,2,1:T(8,128)(2,1)} %get-tuple-element.101) | data formatting | bytes 75497472
  355.9 0.5 broadcast_multiply_fusion
  356.4 0.8 all-gather.2.cloned.1.call-done
  357.2 3.1 reduce_sum.39
  360.3 0.0 copy-done.1
  (4 shorter events, 0.1 us)
Async XLA Ops:
  7.2 26.8 %copy-start = (s32[4,128,64]{1,2,0:T(8,128)S(1)}, s32[4,128,64]{1,2,0:T(8,128)}, u32[]{:S(2)}) copy-start(s32[4,128,64]{1,2,0:T(8,128)} %param.10) | copy-start | bytes 393220
  7.2 212.0 %all-reduce.2.cloned.1.call-start = ((), (), s32[]{:S(2)}) async-start(), calls=%async_computation | async-start | bytes 9437184 | tf_op jit(solution)/shard_map/psum | solution.py:54
  46.5 172.7 %copy-start.4 = (f32[4,2304]{1,0:T(4,128)S(1)}, f32[4,2304]{1,0:T(4,128)}, u32[]{:S(2)}) copy-start(f32[4,2304]{1,0:T(4,128)} %param.12) | copy-start | bytes 110596
  73.4 149.9 %copy-start.2 = (bf16[128,2048]{1,0:T(8,128)(2,1)}, bf16[128,2048]{1,0:T(8,128)(2,1)S(1)}, u32[]{:S(2)}) copy-start(bf16[128,2048]{1,0:T(8,128)(2,1)S(1)} %get-tuple-element.240) | copy-start | bytes 1572868
  73.4 283.8 %all-gather.2.cloned.1.call-start = ((), (), s32[]{:S(2)}) async-start(), calls=%async_computation.1 | async-start | bytes 4325376 | tf_op jit(solution)/shard_map/all_gather | solution.py:76
  297.4 0.7 copy-start.3
  298.0 62.2 %copy-start.1 = (s32[4,128,64]{1,2,0:T(8,128)S(1)}, s32[4,128,64]{1,2,0:T(8,128)}, u32[]{:S(2)}) copy-start(s32[4,128,64]{1,2,0:T(8,128)} %param.10) | copy-start | bytes 393220
Sparse Core Ops, SparseCore 0:
  73.5 145.6 all-reduce.1
  298.2 58.9 all-gather.1
